TPU v7x, 256 devices: a whole 4x4x8 slice. The times are simulated.
256 devices in a mesh: pt: 8 (over x, y_lo), tp: 32 (over y_hi, z, core).
Axes of the slice: x: 4, y: 4 (y_hi: 2, y_lo: 2; y = y_hi * 2 + y_lo), z: 8, core: 2. Of those that a mesh axis runs over, the one named last changes fastest.
Arguments:
- tokens: bfloat16 [4096, 4096], P('pt', 'tp'), may hold values from -6 to 6
- t_values: float32 [8], replicated, may hold values from 0.05 to 0.95
- gate_start: bfloat16 [4096, 14336], P('pt', 'tp'), may hold values from -0.09375 to 0.09375
- gate_bend: bfloat16 [4096, 14336], P('pt', 'tp'), may hold values from -0.1875 to 0.1875
- gate_end: bfloat16 [4096, 14336], P('pt', 'tp'), may hold values from -0.09375 to 0.09375
- up_start: bfloat16 [4096, 14336], P('pt', 'tp'), may hold values from -0.09375 to 0.09375
- up_bend: bfloat16 [4096, 14336], P('pt', 'tp'), may hold values from -0.1875 to 0.1875
- up_end: bfloat16 [4096, 14336], P('pt', 'tp'), may hold values from -0.09375 to 0.09375
- hidden_grad: bfloat16 [4096, 14336], P('pt', 'tp'), may hold values from -6 to 6
Outputs:
- hidden: bfloat16 [4096, 14336], P('pt', 'tp')
- input_grad: bfloat16 [4096, 4096], P('pt', 'tp')
- gate_bend_grad: float32 [4096, 14336], P('pt', 'tp')
- up_bend_grad: float32 [4096, 14336], P('pt', 'tp')
All inputs are finite; a program needn't handle non-finite values.
Results may differ from a plain program's by a relative error of at most 0.014.
Values may be sent and summed in bfloat16 or wider, within the bound.
A program may use at most 128 MiB of HBM per device.

v0:
```python
import jax
import jax.numpy as jnp
from jax import lax
from jax.sharding import PartitionSpec as P


def in_one_piece(arrays, axis, split_dim, concat_dim, along):
    both = jnp.concatenate(arrays, axis=along)
    filled, at, finished = (
        lax.all_to_all(both, axis, split_axis=split_dim, concat_axis=concat_dim, tiled=True),
        0,
        [],
    )
    for a in arrays:
        finished.append(lax.slice_in_dim(filled, at, at + a.shape[along], axis=along))
        at += a.shape[along]
    return tuple(finished)


def cut_along(array, dim, size):
    before, after = (array.shape[:dim], array.shape[dim + 1 :])
    return jnp.moveaxis(array.reshape(*before, size, -1, *after), dim, 0)


def summed_on_arrival(array, axis, dim):
    parts = cut_along(array, dim, lax.axis_size(axis))
    arrived = lax.all_to_all(parts, axis, split_axis=0, concat_axis=0, tiled=True)
    return arrived.astype(jnp.float32).sum(axis=0)


def in_one_piece_2(arrays, axis, dim, along):
    ends, at = ([], 0)
    for a in arrays[:-1]:
        at += a.shape[along]
        ends.append(at)
    both = jnp.concatenate(arrays, axis=along)
    return tuple(
        jnp.split(lax.psum_scatter(both, axis, scatter_dimension=dim, tiled=True), ends, axis=along)
    )


def blend_all(first, middle, last, start, bend, end):
    mixed = (
        first[:, None, None] * start.astype(jnp.float32)[None]
        + middle[:, None, None] * bend.astype(jnp.float32)[None]
        + last[:, None, None] * end.astype(jnp.float32)[None]
    )
    return mixed.astype(jnp.bfloat16)


def per_device(
    tokens, t_values, gate_start, gate_bend, gate_end, up_start, up_bend, up_end, hidden_grad
):
    mine = lax.axis_index("pt")
    first = (1.0 - t_values) ** 2
    middle = 2.0 * t_values * (1.0 - t_values)
    last = t_values * t_values
    gate_parts = blend_all(first, middle, last, gate_start, gate_bend, gate_end)
    up_parts = blend_all(first, middle, last, up_start, up_bend, up_end)
    gate_full, up_full = in_one_piece((gate_parts, up_parts), "pt", 0, 1, 2)
    gate_w = gate_full[0]
    up_w = up_full[0]
    whole = lax.all_gather(tokens, "tp", axis=1, tiled=True)
    gate = jnp.dot(whole, gate_w, preferred_element_type=jnp.float32)
    up = jnp.dot(whole, up_w, preferred_element_type=jnp.float32)
    sig = jax.nn.sigmoid(gate)
    act = gate * sig
    hidden = (act * up).astype(jnp.bfloat16)
    cotf = hidden_grad.astype(jnp.float32)
    d_up = cotf * act
    d_gate = cotf * up * sig * (1.0 + gate * (1.0 - sig))
    d_gate_b = d_gate.astype(jnp.bfloat16)
    d_up_b = d_up.astype(jnp.bfloat16)
    weight_here = lax.dynamic_index_in_dim(middle, mine, 0, keepdims=False)
    scaled_gate = (weight_here * d_gate).astype(jnp.bfloat16)
    scaled_up = (weight_here * d_up).astype(jnp.bfloat16)
    part_gate = lax.dot_general(
        gate_w, d_gate_b, (((1,), (1,)), ((), ())), preferred_element_type=jnp.float32
    )
    part_up = lax.dot_general(
        up_w, d_up_b, (((1,), (1,)), ((), ())), preferred_element_type=jnp.float32
    )
    input_cols = summed_on_arrival((part_gate + part_up).astype(jnp.bfloat16), "tp", 0)
    input_grad = input_cols.T.astype(jnp.bfloat16)
    full_gate = lax.dot_general(
        whole, scaled_gate, (((0,), (0,)), ((), ())), preferred_element_type=jnp.float32
    )
    full_up = lax.dot_general(
        whole, scaled_up, (((0,), (0,)), ((), ())), preferred_element_type=jnp.float32
    )
    gate_grad, up_grad = tuple(
        (
            part.astype(jnp.float32)
            for part in in_one_piece_2(
                (full_gate.astype(jnp.bfloat16), full_up.astype(jnp.bfloat16)), "pt", 0, 1
            )
        )
    )
    return (hidden, input_grad, gate_grad, up_grad)


def solution(mesh):
    return jax.shard_map(
        per_device,
        mesh=mesh,
        in_specs=(
            P("pt", "tp"),
            P(),
            P("pt", "tp"),
            P("pt", "tp"),
            P("pt", "tp"),
            P("pt", "tp"),
            P("pt", "tp"),
            P("pt", "tp"),
            P("pt", "tp"),
        ),
        out_specs=(P("pt", "tp"), P("pt", "tp"), P("pt", "tp"), P("pt", "tp")),
        check_vma=False,
    )
```

profile of v0, /device:TPU:1, one launch (start us, length us, event | category | flops | bytes accessed | tf_op | source)
XLA Modules:
  0.0 382.4 jit_solution(16434651966500397295)
XLA Ops:
  7.2 0.0 copy-start.1
  7.2 0.0 all-gather.2.cloned.1.call-start
  7.2 0.7 all-gather.2.cloned.1.call-update
  7.9 1.2 copy.19
  9.1 1.2 copy.20
  10.4 1.2 copy.21
  11.6 2.2 copy.22
  13.8 2.2 copy.23
  16.0 2.3 copy.24
  18.3 0.0 copy-done.1
  18.3 6.8 %add_convert_fusion.2 = (bf16[8,512,448]{2,1,0:T(8,128)(2,1)}, bf16[8,512,448]{2,1,0:T(8,128)(2,1)}) fusion(f32[512,448]{1,0:T(8,128)S(1)} %copy.21, f32[8]{0:T(128)S(1)} %get-tuple-element.13, f32[512,448]{1,0:T(8,128)S(1)} %copy.20, f32[8]{0:T(128)S(1)} %get-tuple-element.14, f32[512,448]{1,0:T(8,128)S(1)} %copy.19, f32[8]{0:T(128)S(1)} %get-tuple-element.12, ...), kind=kLoop, calls=%fused_computation.2 | loop fusion | flops 22020096 | bytes 12845152 | tf_op jit(solution)/shard_map/convert_element_type | solution.py:48
  25.1 9.4 %pad_maximum_fusion = bf16[8,512,896]{2,1,0:T(8,128)(2,1)} fusion(bf16[8,512,448]{2,1,0:T(8,128)(2,1)} %get-tuple-element.11, bf16[8,512,448]{2,1,0:T(8,128)(2,1)} %get-tuple-element.10), kind=kLoop, calls=%fused_computation.3 | loop fusion | flops 14680064 | bytes 14680064 | tf_op jit(solution)/shard_map/concatenate | solution.py:8
  34.5 5.8 %all-to-all-start = ((bf16[8,512,896]{2,1,0:T(8,128)(2,1)}), bf16[8,512,896]{2,1,0:T(8,128)(2,1)}, u32[]{:S(2)}, u32[]{:S(2)}) async-start(bf16[8,512,896]{2,1,0:T(8,128)(2,1)} %pad_maximum_fusion), calls=%async_computation | async-start | bytes 14680064 | tf_op jit(solution)/shard_map/all_to_all | solution.py:10
  40.3 0.2 reduce-scatter.2.cloned.1.call-start
  40.6 0.6 dynamic_slice.4
  41.2 99.8 %all-to-all-done = bf16[8,512,896]{2,1,0:T(8,128)(2,1)} async-done(((bf16[8,512,896]{2,1,0:T(8,128)(2,1)}), bf16[8,512,896]{2,1,0:T(8,128)(2,1)}, u32[]{:S(2)}, u32[]{:S(2)}) %all-to-all-start) | async-done | bytes 7340064 | tf_op jit(solution)/shard_map/all_to_all | solution.py:10
  141.0 11.6 %all-gather.2.cloned.1.call-done = bf16[512,4096]{1,0:T(8,128)(2,1)} async-done(((bf16[512,128]{1,0:T(8,128)(2,1)}), bf16[512,4096]{1,0:T(8,128)(2,1)}) %all-gather.2.cloned.1.call-update) | async-done | bytes 4194320 | tf_op jit(solution)/shard_map/all_gather | solution.py:63
  152.6 0.0 copy-start.2
  152.6 6.1 %fusion.6 = f32[512,448]{0,1:T(8,128)S(1)} fusion(bf16[512,4096]{1,0:T(8,128)(2,1)} %all-gather.2.cloned.1.call-done, bf16[1,4096,896]{2,1,0:T(8,128)(2,1)} %bitcast), kind=kOutput, calls=%fused_computation.15 | convolution fusion | flops 1879048192 | bytes 9306112 | tf_op jit(solution)/shard_map/dot_general | solution.py:64
  158.7 0.0 copy-done.2
  158.7 0.0 copy-start
  158.8 6.7 %multiply_convert_fusion.2 = (bf16[512,448]{0,1:T(8,128)(2,1)}, f32[512,448]{0,1:T(8,128)S(1)}) fusion(f32[512,448]{0,1:T(8,128)S(1)} %fusion.6, bf16[512,4096]{1,0:T(8,128)(2,1)S(1)} %copy-done.2, bf16[1,4096,896]{2,1,0:T(8,128)(2,1)} %bitcast), kind=kOutput, calls=%fused_computation.22 | convolution fusion | flops 1880424448 | bytes 10682368 | tf_op jit(solution)/shard_map/dot_general | solution.py:65
  165.5 0.0 copy-start.3
  165.5 0.0 copy-done
  165.5 2.8 fusion.1
  168.4 0.0 copy-done.3
  168.4 4.8 %fusion = bf16[4096,448]{0,1:T(8,128)(2,1)} fusion(bf16[512,4096]{1,0:T(8,128)(2,1)S(1)} %copy-done.2, f32[]{:T(128)} %bitcast.7, f32[512,448]{0,1:T(8,128)S(1)} %get-tuple-element.16, bf16[512,448]{0,1:T(8,128)(2,1)S(1)} %copy-done, f32[512,448]{0,1:T(8,128)S(1)} %fusion.6), kind=kOutput, calls=%fused_computation.7 | convolution fusion | flops 1883635712 | bytes 10158084 | tf_op jit(solution)/shard_map/dot_general | solution.py:85
  173.1 6.3 %pad_maximum_fusion.1 = bf16[4096,896]{0,1:T(8,128)(2,1)} fusion(bf16[4096,448]{0,1:T(8,128)(2,1)S(1)} %fusion.1, bf16[4096,448]{0,1:T(8,128)(2,1)} %fusion), kind=kLoop, calls=%fused_computation.4 | loop fusion | flops 14680064 | bytes 14680064 | tf_op jit(solution)/shard_map/concatenate | solution.py:36
  179.4 0.0 copy-start.4
  179.5 0.0 reduce-scatter.2.cloned.1.call-update
  179.5 1.2 copy-done.4
  180.6 5.0 %fusion.2 = f32[4096,512]{1,0:T(8,128)S(1)} fusion(bf16[1,4096,896]{2,1,0:T(8,128)(2,1)} %bitcast, f32[512,448]{0,1:T(8,128)S(1)} %copy-done.4, bf16[512,448]{0,1:T(8,128)(2,1)S(1)} %copy-done, f32[512,448]{0,1:T(8,128)S(1)} %fusion.6), kind=kOutput, calls=%fused_computation.11 | convolution fusion | flops 1881571328 | bytes 14876672 | tf_op jit(solution)/shard_map/dot_general | solution.py:77
  185.6 5.1 %add_convert_fusion = bf16[4096,512]{1,0:T(8,128)(2,1)S(1)} fusion(f32[4096,512]{1,0:T(8,128)S(1)} %fusion.2, bf16[1,4096,896]{2,1,0:T(8,128)(2,1)} %bitcast, bf16[512,448]{0,1:T(8,128)(2,1)S(1)} %copy-done, f32[512,448]{0,1:T(8,128)S(1)} %fusion.6), kind=kOutput, calls=%fused_computation | convolution fusion | flops 1884848128 | bytes 18153472 | tf_op jit(solution)/shard_map/dot_general | solution.py:80
  190.7 99.5 %all_to_all.17 = bf16[32,128,512]{2,1,0:T(8,128)(2,1)} all-to-all(bf16[32,128,512]{2,1,0:T(8,128)(2,1)S(1)} %bitcast.30), channel_id=1, replica_groups=mesh['pt'=8,'tp'=32] {'tp'}, dimensions={0} | all-to-all | bytes 8388608 | tf_op jit(solution)/shard_map/all_to_all | solution.py:27
  290.2 2.9 reduce_sum.12
  293.1 0.8 copy.25
  293.8 79.1 %reduce-scatter.2.cloned.1.call-done = bf16[512,896]{0,1:T(8,128)(2,1)} async-done(((bf16[4096,896]{0,1:T(8,128)(2,1)}), bf16[512,896]{0,1:T(8,128)(2,1)}) %reduce-scatter.2.cloned.1.call-update) | async-done | bytes 917520 | tf_op jit(solution)/shard_map/reduce_scatter | solution.py:38
  372.9 2.6 slice_convert_fusion
  (1 shorter events, 0.0 us)
Async XLA Ops:
  7.2 11.1 %copy-start.1 = (f32[8]{0:T(128)S(1)}, f32[8]{0:T(128)}, u32[]{:S(2)}) copy-start(f32[8]{0:T(128)} %param.10) | copy-start | bytes 100
  7.2 145.4 %all-gather.2.cloned.1.call-start = ((), (), s32[]{:S(2)}) async-start(), calls=%async_computation.3 | async-start | bytes 4325376 | tf_op jit(solution)/shard_map/all_gather | solution.py:63
  34.5 106.4 %all-to-all-start = ((bf16[8,512,896]{2,1,0:T(8,128)(2,1)}), bf16[8,512,896]{2,1,0:T(8,128)(2,1)}, u32[]{:S(2)}, u32[]{:S(2)}) async-start(bf16[8,512,896]{2,1,0:T(8,128)(2,1)} %pad_maximum_fusion), calls=%async_computation | async-start | bytes 14680064 | tf_op jit(solution)/shard_map/all_to_all | solution.py:10
  40.3 332.5 %reduce-scatter.2.cloned.1.call-start = ((), (), s32[]{:S(2)}) async-start(), calls=%async_computation.4 | async-start | bytes 8257536 | tf_op jit(solution)/shard_map/reduce_scatter | solution.py:38
  152.6 6.1 %copy-start.2 = (bf16[512,4096]{1,0:T(8,128)(2,1)S(1)}, bf16[512,4096]{1,0:T(8,128)(2,1)}, u32[]{:S(2)}) copy-start(bf16[512,4096]{1,0:T(8,128)(2,1)} %all-gather.2.cloned.1.call-done) | copy-start | bytes 12582916
  158.7 6.8 %copy-start = (bf16[512,448]{0,1:T(8,128)(2,1)S(1)}, bf16[512,448]{0,1:T(8,128)(2,1)}, u32[]{:S(2)}) copy-start(bf16[512,448]{0,1:T(8,128)(2,1)} %param.17) | copy-start | bytes 1376260
  165.5 2.8 copy-start.3
  179.4 1.2 copy-start.4
Sparse Core Ops, SparseCore 0:
  10.5 142.0 all-gather.1
  179.6 193.2 reduce-scatter.1
where the time goes:
time: 383 us; the launch traced here: 382 us
  waiting for transfers between devices  191 us (50%)
  blocking collectives  99.5 us (26%)
  matrix products  30.5 us (8%)
  other arithmetic  28.1 us (7%)
  between operations  14.1 us (4%)
  local copies, waits for them, and re-layouts  12.9 us (3%)
  starting transfers between devices  6.07 us (2%)
    all_to_all x1, waiting for transfers between devices, in_one_piece(): lax.all_to_all(both, axis, split_axis=split_dim, concat_axis=concat_dim,...  99.8 us
    all_to_all x1, blocking collectives, summed_on_arrival(): lax.all_to_all(parts, axis, split_axis=0, concat_axis=0, tiled=True)  99.5 us
    reduce_scatter x1, waiting for transfers between devices, in_one_piece_2(): lax.psum_scatter(both, axis, scatter_dimension=dim, tiled=True)  79.1 us
    all_gather x1, waiting for transfers between devices, per_device(): whole = lax.all_gather(tokens, 'tp', axis=1, tiled=True)  11.6 us
    concatenate x1, other arithmetic, in_one_piece(): both = jnp.concatenate(arrays, axis=along)  9.45 us
  transfers between devices with their start and end apart: 3, of which 3 were waited for; matrix products, arithmetic and copies ran while one was open for 11% of the time, Pallas kernels for 0%

commit v1 on v0

--- a/solution.py
+++ b/solution.py
@@ -60,7 +60,9 @@
     gate_full, up_full = in_one_piece((gate_parts, up_parts), "pt", 0, 1, 2)
     gate_w = gate_full[0]
     up_w = up_full[0]
-    whole = lax.all_gather(tokens, "tp", axis=1, tiled=True)
+    whole = jnp.concatenate(
+        lax.all_to_all(jnp.stack([tokens] * lax.axis_size("tp")), "tp", 0, 0), axis=1
+    )
     gate = jnp.dot(whole, gate_w, preferred_element_type=jnp.float32)
     up = jnp.dot(whole, up_w, preferred_element_type=jnp.float32)
     sig = jax.nn.sigmoid(gate)

time: 383 us -> 488 us (1.27)
  waiting for transfers between devices: 191 us -> 273 us
  starting transfers between devices: 6.07 us -> 19.4 us
    all_to_all x0 -> x1, waiting for transfers between devices: none -> 95.4 us  [per_device(): lax.all_to_all(jnp.stack([tokens] * lax.axis_size('tp')), 'tp', 0, 0)]
    all_to_all x0 -> x1, starting transfers between devices: none -> 13.2 us  [per_device(): lax.all_to_all(jnp.stack([tokens] * lax.axis_size('tp')), 'tp', 0, 0)]
    all_gather x1 -> x0, waiting for transfers between devices: 11.6 us -> none  [per_device(): whole = lax.all_gather(tokens, 'tp', axis=1, tiled=True)]
  transfers between devices with their start and end apart: 3 -> 3, of which waited for: 3 -> 3; matrix products, arithmetic and copies ran while one was open for 11% -> 3% of each run, Pallas kernels for 0% -> 0%
where the time goes in v1:
time: 488 us; the launch traced here: 487 us
  waiting for transfers between devices  273 us (56%)
  blocking collectives  102 us (21%)
  matrix products  34.4 us (7%)
  other arithmetic  28.7 us (6%)
  starting transfers between devices  19.4 us (4%)
  local copies, waits for them, and re-layouts  15.5 us (3%)
  between operations  14.1 us (3%)
    all_to_all x1, blocking collectives, summed_on_arrival(): lax.all_to_all(parts, axis, split_axis=0, concat_axis=0, tiled=True)  102 us
    all_to_all x1, waiting for transfers between devices, in_one_piece(): lax.all_to_all(both, axis, split_axis=split_dim, concat_axis=concat_dim,...  100 us
    all_to_all x1, waiting for transfers between devices, per_device(): lax.all_to_all(jnp.stack([tokens] * lax.axis_size('tp')), 'tp', 0, 0)  95.4 us
    reduce_scatter x1, waiting for transfers between devices, in_one_piece_2(): lax.psum_scatter(both, axis, scatter_dimension=dim, tiled=True)  77 us
    all_to_all x1, starting transfers between devices, per_device(): lax.all_to_all(jnp.stack([tokens] * lax.axis_size('tp')), 'tp', 0, 0)  13.2 us
  transfers between devices with their start and end apart: 3, of which 3 were waited for; matrix products, arithmetic and copies ran while one was open for 3% of the time, Pallas kernels for 0%

profile of v1, /device:TPU:1, one launch (start us, length us, event | category | flops | bytes accessed | tf_op | source)
XLA Modules:
  0.0 487.2 jit_solution(2278433525755471577)
XLA Ops:
  7.2 0.7 subtract_multiply_fusion
  7.8 1.2 copy.26
  9.1 1.2 copy.27
  10.3 1.2 copy.28
  11.5 2.2 copy.29
  13.7 2.2 copy.30
  15.9 2.3 copy.31
  18.2 6.8 %add_convert_fusion.2 = (bf16[8,512,448]{2,1,0:T(8,128)(2,1)}, bf16[8,512,448]{2,1,0:T(8,128)(2,1)}) fusion(f32[512,448]{1,0:T(8,128)S(1)} %copy.28, f32[8]{0:T(128)S(1)} %get-tuple-element.13, f32[512,448]{1,0:T(8,128)S(1)} %copy.27, f32[8]{0:T(128)S(1)} %get-tuple-element.14, f32[512,448]{1,0:T(8,128)S(1)} %copy.26, f32[8]{0:T(128)S(1)} %get-tuple-element.12, ...), kind=kLoop, calls=%fused_computation.2 | loop fusion | flops 22020096 | bytes 12845152 | tf_op jit(solution)/shard_map/convert_element_type | solution.py:48
  25.0 9.4 %pad_maximum_fusion = bf16[8,512,896]{2,1,0:T(8,128)(2,1)} fusion(bf16[8,512,448]{2,1,0:T(8,128)(2,1)} %get-tuple-element.11, bf16[8,512,448]{2,1,0:T(8,128)(2,1)} %get-tuple-element.10), kind=kLoop, calls=%fused_computation.3 | loop fusion | flops 14680064 | bytes 14680064 | tf_op jit(solution)/shard_map/concatenate | solution.py:8
  34.4 0.0 copy-start.1
  34.4 6.0 %all-to-all-start = ((bf16[8,512,896]{2,1,0:T(8,128)(2,1)}), bf16[8,512,896]{2,1,0:T(8,128)(2,1)}, u32[]{:S(2)}, u32[]{:S(2)}) async-start(bf16[8,512,896]{2,1,0:T(8,128)(2,1)} %pad_maximum_fusion), calls=%async_computation | async-start | bytes 14680064 | tf_op jit(solution)/shard_map/all_to_all | solution.py:10
  40.4 0.0 copy-done.1
  40.4 0.1 copy.32
  40.5 100.4 %all-to-all-done = bf16[8,512,896]{2,1,0:T(8,128)(2,1)} async-done(((bf16[8,512,896]{2,1,0:T(8,128)(2,1)}), bf16[8,512,896]{2,1,0:T(8,128)(2,1)}, u32[]{:S(2)}, u32[]{:S(2)}) %all-to-all-start) | async-done | bytes 7340064 | tf_op jit(solution)/shard_map/all_to_all | solution.py:10
  140.9 2.5 stack.2
  143.4 13.2 %all-to-all-start.1 = ((bf16[32,512,128]{1,2,0:T(8,128)(2,1)}), bf16[32,512,128]{1,2,0:T(8,128)(2,1)}, u32[]{:S(2)}, u32[]{:S(2)}) async-start(bf16[32,512,128]{1,2,0:T(8,128)(2,1)} %stack.2), calls=%async_computation.1 | async-start | bytes 8388608 | tf_op jit(solution)/shard_map/all_to_all | solution.py:64
  156.6 0.2 reduce-scatter.2.cloned.1.call-start
  156.8 0.6 dynamic_slice.4
  157.4 95.4 %all-to-all-done.1 = bf16[32,512,128]{1,2,0:T(8,128)(2,1)} async-done(((bf16[32,512,128]{1,2,0:T(8,128)(2,1)}), bf16[32,512,128]{1,2,0:T(8,128)(2,1)}, u32[]{:S(2)}, u32[]{:S(2)}) %all-to-all-start.1) | async-done | bytes 4194336 | tf_op jit(solution)/shard_map/all_to_all | solution.py:64
  252.8 5.5 %fusion.6 = f32[512,448]{0,1:T(8,128)S(1)} fusion(bf16[512,4096]{0,1:T(8,128)(2,1)} %bitcast.3, bf16[1,4096,896]{2,1,0:T(8,128)(2,1)} %bitcast), kind=kOutput, calls=%fused_computation.15 | convolution fusion | flops 1879048192 | bytes 9306112 | tf_op jit(solution)/shard_map/dot_general | solution.py:66
  258.4 0.0 copy-start
  258.4 7.3 %multiply_convert_fusion.2 = (bf16[512,448]{0,1:T(8,128)(2,1)}, f32[512,448]{0,1:T(8,128)S(1)}) fusion(f32[512,448]{0,1:T(8,128)S(1)} %fusion.6, bf16[512,4096]{0,1:T(8,128)(2,1)} %bitcast.3, bf16[1,4096,896]{2,1,0:T(8,128)(2,1)} %bitcast), kind=kOutput, calls=%fused_computation.22 | convolution fusion | flops 1880424448 | bytes 10682368 | tf_op jit(solution)/shard_map/dot_general | solution.py:67
  265.6 0.0 copy-start.2
  265.6 0.0 copy-done
  265.6 5.0 %fusion.1 = bf16[4096,448]{0,1:T(8,128)(2,1)S(1)} fusion(bf16[512,4096]{0,1:T(8,128)(2,1)} %bitcast.3, bf16[512,448]{0,1:T(8,128)(2,1)S(1)} %copy-done, f32[]{:T(128)} %bitcast.10, f32[512,448]{0,1:T(8,128)S(1)} %fusion.6), kind=kOutput, calls=%fused_computation.8 | convolution fusion | flops 1882718208 | bytes 9240580 | tf_op jit(solution)/shard_map/dot_general | solution.py:90
  270.6 0.0 copy-done.2
  270.6 6.9 %fusion = bf16[4096,448]{0,1:T(8,128)(2,1)} fusion(bf16[512,4096]{0,1:T(8,128)(2,1)} %bitcast.3, f32[]{:T(128)} %bitcast.10, f32[512,448]{0,1:T(8,128)S(1)} %get-tuple-element.16, bf16[512,448]{0,1:T(8,128)(2,1)S(1)} %copy-done, f32[512,448]{0,1:T(8,128)S(1)} %fusion.6), kind=kOutput, calls=%fused_computation.7 | convolution fusion | flops 1883635712 | bytes 10158084 | tf_op jit(solution)/shard_map/dot_general | solution.py:87
  277.5 6.3 %pad_maximum_fusion.1 = bf16[4096,896]{0,1:T(8,128)(2,1)} fusion(bf16[4096,448]{0,1:T(8,128)(2,1)S(1)} %fusion.1, bf16[4096,448]{0,1:T(8,128)(2,1)} %fusion), kind=kLoop, calls=%fused_computation.4 | loop fusion | flops 14680064 | bytes 14680064 | tf_op jit(solution)/shard_map/concatenate | solution.py:36
  283.9 0.0 copy-start.3
  283.9 0.0 reduce-scatter.2.cloned.1.call-update
  283.9 1.2 copy-done.3
  285.0 4.7 fusion.2
  289.8 5.0 %add_convert_fusion = bf16[4096,512]{1,0:T(8,128)(2,1)S(1)} fusion(f32[4096,512]{1,0:T(8,128)S(1)} %fusion.2, bf16[1,4096,896]{2,1,0:T(8,128)(2,1)} %bitcast, bf16[512,448]{0,1:T(8,128)(2,1)S(1)} %copy-done, f32[512,448]{0,1:T(8,128)S(1)} %fusion.6), kind=kOutput, calls=%fused_computation | convolution fusion | flops 1884848128 | bytes 18153472 | tf_op jit(solution)/shard_map/dot_general | solution.py:82
  294.8 102.4 %all_to_all.22 = bf16[32,128,512]{2,1,0:T(8,128)(2,1)} all-to-all(bf16[32,128,512]{2,1,0:T(8,128)(2,1)S(1)} %bitcast.33), channel_id=1, replica_groups=mesh['pt'=8,'tp'=32] {'tp'}, dimensions={0} | all-to-all | bytes 8388608 | tf_op jit(solution)/shard_map/all_to_all | solution.py:27
  397.2 2.8 reduce_sum.12
  400.0 0.8 copy.33
  400.8 77.0 %reduce-scatter.2.cloned.1.call-done = bf16[512,896]{0,1:T(8,128)(2,1)} async-done(((bf16[4096,896]{0,1:T(8,128)(2,1)}), bf16[512,896]{0,1:T(8,128)(2,1)}) %reduce-scatter.2.cloned.1.call-update) | async-done | bytes 917520 | tf_op jit(solution)/shard_map/reduce_scatter | solution.py:38
  477.7 2.6 slice_convert_fusion
Async XLA Ops:
  34.4 6.0 %copy-start.1 = (bf16[512,128]{1,0:T(8,128)(2,1)S(1)}, bf16[512,128]{1,0:T(8,128)(2,1)}, u32[]{:S(2)}) copy-start(bf16[512,128]{1,0:T(8,128)(2,1)} %param.9) | copy-start | bytes 393220
  34.4 106.5 %all-to-all-start = ((bf16[8,512,896]{2,1,0:T(8,128)(2,1)}), bf16[8,512,896]{2,1,0:T(8,128)(2,1)}, u32[]{:S(2)}, u32[]{:S(2)}) async-start(bf16[8,512,896]{2,1,0:T(8,128)(2,1)} %pad_maximum_fusion), calls=%async_computation | async-start | bytes 14680064 | tf_op jit(solution)/shard_map/all_to_all | solution.py:10
  143.4 109.4 %all-to-all-start.1 = ((bf16[32,512,128]{1,2,0:T(8,128)(2,1)}), bf16[32,512,128]{1,2,0:T(8,128)(2,1)}, u32[]{:S(2)}, u32[]{:S(2)}) async-start(bf16[32,512,128]{1,2,0:T(8,128)(2,1)} %stack.2), calls=%async_computation.1 | async-start | bytes 8388608 | tf_op jit(solution)/shard_map/all_to_all | solution.py:64
  156.6 321.1 %reduce-scatter.2.cloned.1.call-start = ((), (), s32[]{:S(2)}) async-start(), calls=%async_computation.4 | async-start | bytes 8257536 | tf_op jit(solution)/shard_map/reduce_scatter | solution.py:38
  258.4 7.3 %copy-start = (bf16[512,448]{0,1:T(8,128)(2,1)S(1)}, bf16[512,448]{0,1:T(8,128)(2,1)}, u32[]{:S(2)}) copy-start(bf16[512,448]{0,1:T(8,128)(2,1)} %param.17) | copy-start | bytes 1376260
  265.6 5.0 %copy-start.2 = (f32[512,448]{0,1:T(8,128)}, f32[512,448]{0,1:T(8,128)S(1)}, u32[]{:S(2)}) copy-start(f32[512,448]{0,1:T(8,128)S(1)} %get-tuple-element.16) | copy-start | bytes 2752516
  283.9 1.2 copy-start.3
Sparse Core Ops, SparseCore 0:
  284.0 193.6 reduce-scatter.1
